TPU v7x, 8 devices: a whole 2x2x1 slice. The times are simulated.
8 devices in a mesh: data: 4 (over z, y, x), stage: 2 (over core).
Axes of the slice: x: 2, y: 2, z: 1, core: 2. Of those that a mesh axis runs over, the one named last changes fastest.
Arguments:
- act_in: bfloat16 [4, 4, 64, 2048], P(None, 'data')
- cot_out: bfloat16 [4, 4, 64, 2048], P(None, 'data')
- seq_lens: int32 [4, 4], P(None, 'data')
- w_gate: bfloat16 [2, 2, 2048, 5632], P('stage', None, 'data')
- w_in: bfloat16 [2, 2, 2048, 5632], P('stage', None, 'data')
- w_out: bfloat16 [2, 2, 5632, 2048], P('stage', None, 'data')
Outputs:
- output 1: bfloat16 [4, 4, 64, 2048], P(None, 'data')
- output 2: float32 [2, 2, 2048, 5632], P('stage', None, 'data')
- output 3: float32 [2, 2, 2048, 5632], P('stage', None, 'data')
- output 4: float32 [2, 2, 5632, 2048], P('stage', None, 'data')
All inputs are finite; a program needn't handle non-finite values.
Results may differ from a plain program's by a relative error of at most 0.02.
Values are sent between devices in bfloat16 or wider.
A program may use at most 1 GiB of HBM per device.

v0:
```python
import jax
import jax.numpy as jnp
from jax import lax
from jax.sharding import PartitionSpec as P

EPSILON = 1e-6


def tn_dot(left, right):
    return lax.dot_general(left, right, (((0,), (0,)), ((), ())), preferred_element_type=jnp.float32)


def nt_dot(left, right):
    return lax.dot_general(left, right, (((1,), (1,)), ((), ())), preferred_element_type=jnp.float32)


def norm_fwd(h_act):
    h_wide = h_act.astype(jnp.float32)
    inv_rms = lax.rsqrt(jnp.mean(h_wide * h_wide, axis=-1, keepdims=True) + EPSILON)
    return h_wide, inv_rms, (h_wide * inv_rms).astype(jnp.bfloat16)


def layer_fwd(h_act, keep_mask, w_gate, w_in, w_out):
    h_wide, inv_rms, normed = norm_fwd(h_act)
    gate_pre = jnp.dot(normed, w_gate, preferred_element_type=jnp.float32)
    in_pre = jnp.dot(normed, w_in, preferred_element_type=jnp.float32)
    hidden = (gate_pre * jax.nn.sigmoid(gate_pre) * in_pre).astype(jnp.bfloat16)
    branch = jnp.dot(hidden, w_out, preferred_element_type=jnp.float32).astype(jnp.bfloat16)
    return (h_wide + keep_mask * branch.astype(jnp.float32)).astype(jnp.bfloat16)


def layer_bwd(h_act, keep_mask, w_gate, w_in, w_out, d_next):
    h_wide, inv_rms, normed = norm_fwd(h_act)
    gate_pre = jnp.dot(normed, w_gate, preferred_element_type=jnp.float32)
    in_pre = jnp.dot(normed, w_in, preferred_element_type=jnp.float32)
    gate_sig = jax.nn.sigmoid(gate_pre)
    gate_act = gate_pre * gate_sig
    hidden = (gate_act * in_pre).astype(jnp.bfloat16)
    d_wide = d_next.astype(jnp.float32)
    d_branch = (keep_mask * d_wide).astype(jnp.bfloat16)
    grad_out = tn_dot(hidden, d_branch)
    d_hidden = nt_dot(d_branch, w_out)
    d_gate = (d_hidden * in_pre * gate_sig * (1.0 + gate_pre * (1.0 - gate_sig))).astype(jnp.bfloat16)
    d_in = (d_hidden * gate_act).astype(jnp.bfloat16)
    grad_gate = tn_dot(normed, d_gate)
    grad_in = tn_dot(normed, d_in)
    d_normed = nt_dot(d_gate, w_gate) + nt_dot(d_in, w_in)
    d_resid = inv_rms * d_normed - h_wide * (inv_rms * inv_rms * inv_rms) * jnp.mean(d_normed * h_wide, axis=-1, keepdims=True)
    return (d_wide + d_resid).astype(jnp.bfloat16), grad_gate, grad_in, grad_out


def solution(mesh):
    n_stage = mesh.shape['stage']
    fwd_perm = [(src_idx, src_idx + 1) for src_idx in range(n_stage - 1)]
    bwd_perm = [(src_idx + 1, src_idx) for src_idx in range(n_stage - 1)]
    act_spec = P(None, 'data')
    weight_spec = P('stage', None, 'data', None)

    def local_step(act_in, cot_out, seq_lens, w_gate, w_in, w_out):
        n_micro, n_rows, seq_len, d_model = act_in.shape
        tokens = n_rows * seq_len
        stage_id = lax.axis_index('stage')
        gate_full = lax.all_gather(w_gate[0], 'data', axis=1, tiled=True)
        in_full = lax.all_gather(w_in[0], 'data', axis=1, tiled=True)
        out_full = lax.all_gather(w_out[0], 'data', axis=1, tiled=True)
        n_layer, d_model_w, d_ff = gate_full.shape
        keep_all = (jnp.arange(seq_len)[None, None, :] < seq_lens[:, :, None]).astype(jnp.float32).reshape(n_micro, tokens, 1)
        act_flat = act_in.reshape(n_micro, tokens, d_model)
        cot_flat = cot_out.reshape(n_micro, tokens, d_model)
        n_steps = n_micro + n_stage - 1

        def fwd_step(step_idx, loop_carry):
            recv_act, act_stash = loop_carry
            micro_idx = step_idx - stage_id
            is_valid = (micro_idx >= 0) & (micro_idx < n_micro)
            micro_pos = jnp.clip(micro_idx, 0, n_micro - 1)
            keep_mask = lax.dynamic_index_in_dim(keep_all, micro_pos, 0, keepdims=False)
            first_act = lax.dynamic_index_in_dim(act_flat, micro_pos, 0, keepdims=False)
            h_act = jnp.where(stage_id == 0, first_act, recv_act)

            def run_layers(operands):
                h_cur, stash_cur = operands
                for layer_idx in range(n_layer):
                    stash_cur = lax.dynamic_update_slice(stash_cur, h_cur[None, None], (micro_pos, layer_idx, 0, 0))
                    h_cur = layer_fwd(h_cur, keep_mask, gate_full[layer_idx], in_full[layer_idx], out_full[layer_idx])
                return h_cur, stash_cur

            h_out, act_stash = lax.cond(is_valid, run_layers, lambda operands: operands, (h_act, act_stash))
            return lax.ppermute(h_out, 'stage', fwd_perm), act_stash

        zero_act = jnp.zeros((tokens, d_model), jnp.bfloat16)
        stash_init = jnp.zeros((n_micro, n_layer, tokens, d_model), jnp.bfloat16)
        last_act, act_stash = lax.fori_loop(0, n_steps, fwd_step, (zero_act, stash_init))

        def bwd_step(step_idx, loop_carry):
            recv_cot, dx_buf, gate_acc, in_acc, out_acc = loop_carry
            micro_idx = step_idx - (n_stage - 1 - stage_id)
            is_valid = (micro_idx >= 0) & (micro_idx < n_micro)
            micro_pos = jnp.clip(micro_idx, 0, n_micro - 1)
            keep_mask = lax.dynamic_index_in_dim(keep_all, micro_pos, 0, keepdims=False)
            top_cot = (lax.dynamic_index_in_dim(cot_flat, micro_pos, 0, keepdims=False).astype(jnp.float32) * keep_mask).astype(jnp.bfloat16)
            d_act = jnp.where(stage_id == n_stage - 1, top_cot, recv_cot)

            def run_layers(operands):
                d_cur, gate_sums, in_sums, out_sums = operands
                gate_list, in_list, out_list = list(gate_sums), list(in_sums), list(out_sums)
                for layer_idx in reversed(range(n_layer)):
                    h_saved = lax.dynamic_slice(act_stash, (micro_pos, layer_idx, 0, 0), (1, 1, tokens, d_model)).reshape(tokens, d_model)
                    d_cur, part_gate, part_in, part_out = layer_bwd(h_saved, keep_mask, gate_full[layer_idx], in_full[layer_idx], out_full[layer_idx], d_cur)
                    gate_list[layer_idx] = gate_list[layer_idx] + part_gate
                    in_list[layer_idx] = in_list[layer_idx] + part_in
                    out_list[layer_idx] = out_list[layer_idx] + part_out
                return d_cur, tuple(gate_list), tuple(in_list), tuple(out_list)

            d_out, gate_acc, in_acc, out_acc = lax.cond(is_valid, run_layers, lambda operands: operands, (d_act, gate_acc, in_acc, out_acc))
            old_rows = lax.dynamic_index_in_dim(dx_buf, micro_pos, 0, keepdims=True)
            new_rows = jnp.where(is_valid & (stage_id == 0), d_out[None], old_rows)
            dx_buf = lax.dynamic_update_index_in_dim(dx_buf, new_rows, micro_pos, 0)
            return lax.ppermute(d_out, 'stage', bwd_perm), dx_buf, gate_acc, in_acc, out_acc

        zero_gate = tuple(jnp.zeros((d_model, d_ff), jnp.float32) for layer_idx in range(n_layer))
        zero_out = tuple(jnp.zeros((d_ff, d_model), jnp.float32) for layer_idx in range(n_layer))
        bwd_init = (zero_act, jnp.zeros((n_micro, tokens, d_model), jnp.bfloat16), zero_gate, zero_gate, zero_out)
        last_cot, dx_buf, gate_acc, in_acc, out_acc = lax.fori_loop(0, n_steps, bwd_step, bwd_init)
        act_grad = lax.psum(dx_buf, 'stage').reshape(n_micro, n_rows, seq_len, d_model)
        gate_grad = lax.psum_scatter(jnp.stack(gate_acc), 'data', scatter_dimension=1, tiled=True)[None]
        in_grad = lax.psum_scatter(jnp.stack(in_acc), 'data', scatter_dimension=1, tiled=True)[None]
        out_grad = lax.psum_scatter(jnp.stack(out_acc), 'data', scatter_dimension=1, tiled=True)[None]
        return act_grad, gate_grad, in_grad, out_grad

    return jax.shard_map(local_step, mesh=mesh, in_specs=(act_spec, act_spec, act_spec, weight_spec, weight_spec, weight_spec), out_specs=(act_spec, weight_spec, weight_spec, weight_spec), check_vma=False)
```

profile of v0, /device:TPU:0, one launch (start us, length us, event | category | flops | bytes accessed | tf_op | source)
XLA Modules:
  0.0 5497.7 jit_solution(4879882152517977975)
XLA Ops:
  10.1 400.1 %all-gather.7.cloned.1.call-done = bf16[1,2,2048,5632]{3,2,1,0:T(8,128)(2,1)} async-done(((bf16[1,2,512,5632]{3,2,1,0:T(8,128)(2,1)}), bf16[1,2,2048,5632]{3,2,1,0:T(8,128)(2,1)}) %all-gather.7.cloned.1.call-update) | async-done | bytes 46137360 | tf_op jit(solution)/shard_map/all_gather | solution.py:63
  410.1 399.3 %all-gather.9.cloned.1.call-done = bf16[1,2,2048,5632]{3,2,1,0:T(8,128)(2,1)} async-done(((bf16[1,2,512,5632]{3,2,1,0:T(8,128)(2,1)}), bf16[1,2,2048,5632]{3,2,1,0:T(8,128)(2,1)}) %all-gather.9.cloned.1.call-update) | async-done | bytes 46137360 | tf_op jit(solution)/shard_map/all_gather | solution.py:64
  809.5 399.3 %all-gather.11.cloned.1.call-done = bf16[1,2,5632,2048]{3,2,1,0:T(8,128)(2,1)} async-done(((bf16[1,2,1408,2048]{3,2,1,0:T(8,128)(2,1)}), bf16[1,2,5632,2048]{3,2,1,0:T(8,128)(2,1)}) %all-gather.11.cloned.1.call-update) | async-done | bytes 46137360 | tf_op jit(solution)/shard_map/all_gather | solution.py:65
  1210.4 328.9 %while.47 = (s32[]{:T(128)}, bf16[64,2048]{1,0:T(8,128)(2,1)S(1)}, bf16[4,2,64,2048]{3,2,1,0:T(8,128)(2,1)}, s32[]{:T(128)}, pred[]{:T(512)}, /*index=5*/bf16[4,...) while((s32[]{:T(128)}, bf16[64,2048]{1,0:T(8,128)(2,1)S(1)}, ...), condition=%wide.region_5.6_spmd.clone, body=%wide.region_0.5_spmd.clone.sunk | while | flops 8866759680 | bytes 152310656 | solution.py:93
  1211.5 61.5 %conditional.6 = (bf16[64,2048]{1,0:T(8,128)(2,1)S(1)}, bf16[4,2,64,2048]{3,2,1,0:T(8,128)(2,1)}) conditional(s32[]{:T(128)} %convert_element_type.381, (bf16[64,2048]{1,0:T(8,128)(2,1)S(1)}, bf16[4,2,64,2048]{3,2,1,0:T(8,128)(2,1)}) %tuple.116, (bf16[64,2048]{1,0:T(8,128)(2,1)S(1)}, f32[4,64,1]{1,2,0:T(1,128)S(1)}, s32[]{:T(128)}, ...), branch_computations={%region_1.1_spmd, %region_2.4_spmd} | conditional | flops 8866627584 | bytes 150474304 | solution.py:88
  1276.4 61.5 %conditional.6 = (bf16[64,2048]{1,0:T(8,128)(2,1)S(1)}, bf16[4,2,64,2048]{3,2,1,0:T(8,128)(2,1)}) conditional(s32[]{:T(128)} %convert_element_type.381, (bf16[64,2048]{1,0:T(8,128)(2,1)S(1)}, bf16[4,2,64,2048]{3,2,1,0:T(8,128)(2,1)}) %tuple.116, (bf16[64,2048]{1,0:T(8,128)(2,1)S(1)}, f32[4,64,1]{1,2,0:T(1,128)S(1)}, s32[]{:T(128)}, ...), branch_computations={%region_1.1_spmd, %region_2.4_spmd} | conditional | flops 8866627584 | bytes 150474304 | solution.py:88
  1342.4 61.5 %conditional.6 = (bf16[64,2048]{1,0:T(8,128)(2,1)S(1)}, bf16[4,2,64,2048]{3,2,1,0:T(8,128)(2,1)}) conditional(s32[]{:T(128)} %convert_element_type.381, (bf16[64,2048]{1,0:T(8,128)(2,1)S(1)}, bf16[4,2,64,2048]{3,2,1,0:T(8,128)(2,1)}) %tuple.116, (bf16[64,2048]{1,0:T(8,128)(2,1)S(1)}, f32[4,64,1]{1,2,0:T(1,128)S(1)}, s32[]{:T(128)}, ...), branch_computations={%region_1.1_spmd, %region_2.4_spmd} | conditional | flops 8866627584 | bytes 150474304 | solution.py:88
  1408.4 61.5 %conditional.6 = (bf16[64,2048]{1,0:T(8,128)(2,1)S(1)}, bf16[4,2,64,2048]{3,2,1,0:T(8,128)(2,1)}) conditional(s32[]{:T(128)} %convert_element_type.381, (bf16[64,2048]{1,0:T(8,128)(2,1)S(1)}, bf16[4,2,64,2048]{3,2,1,0:T(8,128)(2,1)}) %tuple.116, (bf16[64,2048]{1,0:T(8,128)(2,1)S(1)}, f32[4,64,1]{1,2,0:T(1,128)S(1)}, s32[]{:T(128)}, ...), branch_computations={%region_1.1_spmd, %region_2.4_spmd} | conditional | flops 8866627584 | bytes 150474304 | solution.py:88
  1474.5 63.7 %collective-permute-start.1 = (bf16[64,2048]{1,0:T(8,128)(2,1)S(1)}, bf16[64,2048]{1,0:T(8,128)(2,1)S(1)}, u32[]{:S(2)}, u32[]{:S(2)}) collective-permute-start(bf16[64,2048]{1,0:T(8,128)(2,1)S(1)} %get-tuple-element.1056), channel_id=1, source_target_pairs={{0,1},{2,3},{4,5},{6,7}} | collective-permute-start | bytes 786440 | tf_op jit(solution)/shard_map/while/body/eval_jaxpr/ppermute | solution.py:89
  1555.5 15.4 broadcast.135.clone.2
  1586.1 15.3 broadcast.135.clone
  1616.4 15.3 broadcast.135
  1631.7 1523.7 %while.46 = (s32[]{:T(128)}, bf16[64,2048]{1,0:T(8,128)(2,1)S(1)}, bf16[4,64,2048]{2,1,0:T(8,128)(2,1)}, f32[2048,5632]{1,0:T(8,128)}, f32[2048,5632]{1,0:T(8,12...) while((s32[]{:T(128)}, bf16[64,2048]{1,0:T(8,128)(2,1)S(1)}, ...), condition=%wide.region_13.14_spmd, body=%wide.region_6.13_spmd.sunk | while | flops 23714529280 | bytes 849359424 | solution.py:124
  1658.7 294.0 %collective-permute-done = bf16[64,2048]{1,0:T(8,128)(2,1)S(1)} collective-permute-done((bf16[64,2048]{1,0:T(8,128)(2,1)}, bf16[64,2048]{1,0:T(8,128)(2,1)S(1)}, u32[]{:S(2)}, u32[]{:S(2)}) %collective-permute-start) | collective-permute-done | bytes 262176 | tf_op jit(solution)/shard_map/while/body/eval_jaxpr/ppermute | solution.py:119
  1955.0 295.1 %conditional.5 = (bf16[64,2048]{1,0:T(8,128)(2,1)}, f32[2048,5632]{1,0:T(8,128)}, f32[2048,5632]{1,0:T(8,128)}, f32[2048,5632]{1,0:T(8,128)}, f32[2048,5632]{1,0...) conditional(s32[]{:T(128)} %convert_element_type.379, ...), branch_computations={%region_7.7_spmd, %region_8.12_spmd} | conditional | flops 23713873920 | bytes 846735680 | solution.py:115
  2074.0 29.1 convolution_add_fusion.5
  2103.1 29.2 convolution_add_fusion.4
  2133.2 29.0 convolution_add_fusion.1
  2162.2 29.5 convolution_add_fusion.3
  2191.7 29.4 convolution_add_fusion
  2221.1 29.0 convolution_add_fusion.2
  2255.9 294.9 %conditional.5 = (bf16[64,2048]{1,0:T(8,128)(2,1)}, f32[2048,5632]{1,0:T(8,128)}, f32[2048,5632]{1,0:T(8,128)}, f32[2048,5632]{1,0:T(8,128)}, f32[2048,5632]{1,0...) conditional(s32[]{:T(128)} %convert_element_type.379, ...), branch_computations={%region_7.7_spmd, %region_8.12_spmd} | conditional | flops 23713873920 | bytes 846735680 | solution.py:115
  2375.0 29.1 convolution_add_fusion.5
  2404.0 29.2 convolution_add_fusion.4
  2434.2 29.0 convolution_add_fusion.1
  2463.2 29.5 convolution_add_fusion.3
  2492.6 29.1 convolution_add_fusion
  2521.7 29.0 convolution_add_fusion.2
  2556.5 294.7 %conditional.5 = (bf16[64,2048]{1,0:T(8,128)(2,1)}, f32[2048,5632]{1,0:T(8,128)}, f32[2048,5632]{1,0:T(8,128)}, f32[2048,5632]{1,0:T(8,128)}, f32[2048,5632]{1,0...) conditional(s32[]{:T(128)} %convert_element_type.379, ...), branch_computations={%region_7.7_spmd, %region_8.12_spmd} | conditional | flops 23713873920 | bytes 846735680 | solution.py:115
  2675.5 29.1 convolution_add_fusion.5
  2704.5 29.2 convolution_add_fusion.4
  2734.7 29.0 convolution_add_fusion.1
  2763.7 29.5 convolution_add_fusion.3
  2793.1 29.1 convolution_add_fusion
  2822.2 29.0 convolution_add_fusion.2
  2856.9 295.1 %conditional.5 = (bf16[64,2048]{1,0:T(8,128)(2,1)}, f32[2048,5632]{1,0:T(8,128)}, f32[2048,5632]{1,0:T(8,128)}, f32[2048,5632]{1,0:T(8,128)}, f32[2048,5632]{1,0...) conditional(s32[]{:T(128)} %convert_element_type.379, ...), branch_computations={%region_7.7_spmd, %region_8.12_spmd} | conditional | flops 23713873920 | bytes 846735680 | solution.py:115
  2975.9 29.1 convolution_add_fusion.5
  3005.0 29.2 convolution_add_fusion.4
  3035.1 29.0 convolution_add_fusion.1
  3064.1 29.5 convolution_add_fusion.3
  3093.6 29.4 convolution_add_fusion
  3123.0 29.0 convolution_add_fusion.2
  3155.5 59.6 %pad_maximum_fusion.2 = f32[2,5632,2048]{2,1,0:T(8,128)} fusion(f32[1,5632,2048]{2,1,0:T(8,128)} %bitcast.190, f32[1,5632,2048]{2,1,0:T(8,128)} %bitcast.191), kind=kLoop, calls=%fused_computation.158 | loop fusion | flops 23068672 | bytes 184549376 | tf_op jit(solution)/shard_map/stack | solution.py:128
  3215.2 61.3 %pad_maximum_fusion = f32[2,2048,5632]{2,1,0:T(8,128)} fusion(f32[1,2048,5632]{2,1,0:T(8,128)} %bitcast.194, f32[1,2048,5632]{2,1,0:T(8,128)} %bitcast.195), kind=kLoop, calls=%fused_computation.156 | loop fusion | flops 23068672 | bytes 184549376 | tf_op jit(solution)/shard_map/stack | solution.py:126
  3276.5 61.3 %pad_maximum_fusion.1 = f32[2,2048,5632]{2,1,0:T(8,128)} fusion(f32[1,2048,5632]{2,1,0:T(8,128)} %bitcast.192, f32[1,2048,5632]{2,1,0:T(8,128)} %bitcast.193), kind=kLoop, calls=%fused_computation.157 | loop fusion | flops 23068672 | bytes 184549376 | tf_op jit(solution)/shard_map/stack | solution.py:127
  3337.9 632.9 %reduce-scatter.8.cloned.1.call-done = f32[2,1408,2048]{2,1,0:T(8,128)} async-done(((f32[2,5632,2048]{2,1,0:T(8,128)}), f32[2,1408,2048]{2,1,0:T(8,128)}) %reduce-scatter.8.cloned.1.call-update) | async-done | bytes 23068688 | tf_op jit(solution)/shard_map/reduce_scatter | solution.py:128
  3970.8 758.6 %reduce-scatter.4.cloned.1.call-done = f32[2,512,5632]{2,1,0:T(8,128)} async-done(((f32[2,2048,5632]{2,1,0:T(8,128)}), f32[2,512,5632]{2,1,0:T(8,128)}) %reduce-scatter.4.cloned.1.call-update) | async-done | bytes 23068688 | tf_op jit(solution)/shard_map/reduce_scatter | solution.py:126
  4729.4 758.8 %reduce-scatter.6.cloned.1.call-done = f32[2,512,5632]{2,1,0:T(8,128)} async-done(((f32[2,2048,5632]{2,1,0:T(8,128)}), f32[2,512,5632]{2,1,0:T(8,128)}) %reduce-scatter.6.cloned.1.call-update) | async-done | bytes 23068688 | tf_op jit(solution)/shard_map/reduce_scatter | solution.py:127
  (274 shorter events, 826.8 us)
Async XLA Ops:
  7.2 403.0 %all-gather.7.cloned.1.call-start = ((), (), s32[]{:S(2)}) async-start(), calls=%async_computation.7 | async-start | bytes 57671680 | tf_op jit(solution)/shard_map/all_gather | solution.py:63
  7.9 801.6 %all-gather.9.cloned.1.call-start = ((), (), s32[]{:S(2)}) async-start(), calls=%async_computation.8 | async-start | bytes 57671680 | tf_op jit(solution)/shard_map/all_gather | solution.py:64
  8.7 1200.1 %all-gather.11.cloned.1.call-start = ((), (), s32[]{:S(2)}) async-start(), calls=%async_computation.9 | async-start | bytes 57671680 | tf_op jit(solution)/shard_map/all_gather | solution.py:65
  9.4 3328.5 %all-reduce.2.cloned.1.call-start = ((), (), s32[]{:S(2)}) async-start(), calls=%async_computation.3 | async-start | bytes 2097152 | tf_op jit(solution)/shard_map/psum | solution.py:125
  1273.0 2.4 collective-permute-start.1
  1338.0 3.4 collective-permute-start.1
  1404.0 3.4 collective-permute-start.1
  1469.9 3.4 collective-permute-start.1
  1474.5 64.9 %collective-permute-start.1 = (bf16[64,2048]{1,0:T(8,128)(2,1)S(1)}, bf16[64,2048]{1,0:T(8,128)(2,1)S(1)}, u32[]{:S(2)}, u32[]{:S(2)}) collective-permute-start(bf16[64,2048]{1,0:T(8,128)(2,1)S(1)} %get-tuple-element.1056), channel_id=1, source_target_pairs={{0,1},{2,3},{4,5},{6,7}} | collective-permute-start | bytes 786440 | tf_op jit(solution)/shard_map/while/body/eval_jaxpr/ppermute | solution.py:89
  1655.7 297.0 %collective-permute-start = (bf16[64,2048]{1,0:T(8,128)(2,1)}, bf16[64,2048]{1,0:T(8,128)(2,1)S(1)}, u32[]{:S(2)}, u32[]{:S(2)}) collective-permute-start(bf16[64,2048]{1,0:T(8,128)(2,1)} %get-tuple-element.1038), channel_id=1, source_target_pairs={{1,0},{3,2},{5,4},{7,6}} | collective-permute-start | bytes 786440 | tf_op jit(solution)/shard_map/while/body/eval_jaxpr/ppermute | solution.py:119
  1956.2 56.0 %copy-start.8 = (f32[64]{0:T(128)}, f32[64]{0:T(128)S(1)}, u32[]{:S(2)}) copy-start(f32[64]{0:T(128)S(1)} %get-tuple-element.863) | copy-start | bytes 772 | tf_op jit(solution)/shard_map/while/body/eval_jaxpr/cond
  2060.2 13.8 copy-start
  2103.1 30.1 copy-start.7
  2133.2 29.0 copy-start.5
  2162.2 29.5 copy-start.4
  2162.2 29.5 copy-start.9
  2191.7 29.4 copy-start.2
  2250.1 3.4 collective-permute-start
  2257.0 56.1 %copy-start.8 = (f32[64]{0:T(128)}, f32[64]{0:T(128)S(1)}, u32[]{:S(2)}) copy-start(f32[64]{0:T(128)S(1)} %get-tuple-element.863) | copy-start | bytes 772 | tf_op jit(solution)/shard_map/while/body/eval_jaxpr/cond
  2348.9 12.3 copy-start.6
  2361.2 13.8 copy-start
  2404.0 30.1 copy-start.7
  2434.2 29.0 copy-start.5
  2463.1 29.5 copy-start.4
  2463.2 29.5 copy-start.9
  2492.6 29.1 copy-start.2
  2550.7 3.4 collective-permute-start
  2557.6 56.0 %copy-start.8 = (f32[64]{0:T(128)}, f32[64]{0:T(128)S(1)}, u32[]{:S(2)}) copy-start(f32[64]{0:T(128)S(1)} %get-tuple-element.863) | copy-start | bytes 772 | tf_op jit(solution)/shard_map/while/body/eval_jaxpr/cond
  2649.4 12.3 copy-start.6
  2661.7 13.8 copy-start
  2704.5 30.1 copy-start.7
  2734.7 29.0 copy-start.5
  2763.6 29.5 copy-start.4
  2763.6 29.5 copy-start.9
  2793.1 29.1 copy-start.2
  2851.2 3.4 collective-permute-start
  2858.1 56.0 %copy-start.8 = (f32[64]{0:T(128)}, f32[64]{0:T(128)S(1)}, u32[]{:S(2)}) copy-start(f32[64]{0:T(128)S(1)} %get-tuple-element.863) | copy-start | bytes 772 | tf_op jit(solution)/shard_map/while/body/eval_jaxpr/cond
  2949.8 12.3 copy-start.6
  2962.1 13.8 copy-start
  3005.0 30.1 copy-start.7
  3035.1 29.0 copy-start.5
  3064.1 29.5 copy-start.4
  3064.1 29.5 copy-start.9
  3093.5 29.4 copy-start.2
  3152.0 3.4 collective-permute-start
  3155.4 815.4 %reduce-scatter.8.cloned.1.call-start = ((), (), s32[]{:S(2)}) async-start(), calls=%async_computation.6 | async-start | bytes 115343360 | tf_op jit(solution)/shard_map/reduce_scatter | solution.py:128
  3215.2 1514.3 %reduce-scatter.4.cloned.1.call-start = ((), (), s32[]{:S(2)}) async-start(), calls=%async_computation.4 | async-start | bytes 115343360 | tf_op jit(solution)/shard_map/reduce_scatter | solution.py:126
  3276.5 2211.7 %reduce-scatter.6.cloned.1.call-start = ((), (), s32[]{:S(2)}) async-start(), calls=%async_computation.5 | async-start | bytes 115343360 | tf_op jit(solution)/shard_map/reduce_scatter | solution.py:127
  (10 other events, 110.3 us)
Sparse Core Ops, SparseCore 0:
  9.8 400.3 all-gather.6
  411.9 397.4 all-gather.8
  811.3 397.4 all-gather.10
  3155.6 13.8 all-reduce.1
  3215.3 755.4 reduce-scatter.7
  3974.3 755.1 reduce-scatter.3
  4733.0 755.1 reduce-scatter.5
where the time goes:
time: 5510 us; the launch traced here: 5500 us
  waiting for transfers between devices  3650 us (66%)
  matrix products  1400 us (25%)
  other arithmetic  220 us (4%)
  local copies, waits for them, and re-layouts  113 us (2%)
  starting transfers between devices  78.6 us (1%)
    reduce_scatter x1, waiting for transfers between devices, local_step(): lax.psum_scatter(jnp.stack(in_acc), 'data', scatter_dimension=1, tiled=True)  759 us
    reduce_scatter x1, waiting for transfers between devices, local_step(): lax.psum_scatter(jnp.stack(gate_acc), 'data', scatter_dimension=1, tiled=...  759 us
    dot_general x24, matrix products, tn_dot(): lax.dot_general(left, right, (((0,), (0,)), ((), ())), preferred_element_...  700 us
    reduce_scatter x1, waiting for transfers between devices, local_step(): lax.psum_scatter(jnp.stack(out_acc), 'data', scatter_dimension=1, tiled=T...  633 us
    all_gather x1, waiting for transfers between devices, local_step(): gate_full = lax.all_gather(w_gate[0], 'data', axis=1, tiled=True)  400 us
    all_gather x1, waiting for transfers between devices, local_step(): out_full = lax.all_gather(w_out[0], 'data', axis=1, tiled=True)  399 us
    all_gather x1, waiting for transfers between devices, local_step(): in_full = lax.all_gather(w_in[0], 'data', axis=1, tiled=True)  399 us
    dot_general x24, matrix products, nt_dot(): lax.dot_general(left, right, (((1,), (1,)), ((), ())), preferred_element_...  297 us
  transfers between devices with their start and end apart: 17, of which 16 were waited for; matrix products, arithmetic and copies ran while one was open for 3% of the time, Pallas kernels for 0%

commit v1 on v0

v1 whole, which is shorter than its diff:
```python
import functools

import jax
import jax.numpy as jnp
from jax import lax
from jax.experimental import pallas as pl
from jax.experimental.pallas import tpu as pltpu
from jax.sharding import PartitionSpec as P

EPSILON = 1e-6
MESH = pl.DeviceIdType.MESH
BF16, F32 = jnp.bfloat16, jnp.float32
LANES = 128
VMEM_LIMIT = 67043328


def nt_dot(left, right):
    return lax.dot_general(left, right, (((1,), (1,)), ((), ())), preferred_element_type=F32)


def place():
    d = lax.axis_index('data')
    s = lax.axis_index('stage')
    x = lax.rem(d, 2)
    y = lax.div(d, 2)
    return d, s, 2 * y + 1 - x, 2 * (1 - y) + x, 3 - d


def meet():
    d, s, xn, yn, dg = place()
    barrier = pltpu.get_barrier_semaphore()
    for chip, core in ((xn, s), (yn, s), (dg, s), (xn, 1 - s), (yn, 1 - s), (dg, 1 - s), (d, 1 - s)):
        pl.semaphore_signal(barrier, inc=1, device_id=(chip, core), device_id_type=MESH)
    pl.semaphore_wait(barrier, 7)


def remote(src, dst, send_sem, recv_sem, device):
    return pltpu.make_async_remote_copy(src_ref=src, dst_ref=dst, send_sem=send_sem, recv_sem=recv_sem, device_id=device, device_id_type=MESH)


def gather_kernel(act, cot, lens, w_gate, w_in, inp_all, lens_all, gate_in, in_in, other, ss, rs, ls):
    d, s, xn, yn, dg = place()
    rows, cols = act.shape[0], gate_in.shape[2]
    half = rows // 2
    meet()
    own_lens = pltpu.make_async_copy(lens, lens_all.at[d], ls.at[0])
    own_lens.start()
    len_sends = [remote(lens, lens_all.at[d], ss.at[4 + i], rs.at[4 + i], (chip, s)) for i, chip in enumerate((xn, yn, dg))]
    for copy in len_sends:
        copy.start()

    def own_sends(src):
        return [remote(src, inp_all.at[d], ss.at[i], rs.at[i], (chip, s)) for i, chip in enumerate((xn, yn))]

    def start_own(src):
        for copy in own_sends(src):
            copy.start()
        pltpu.make_async_copy(src, inp_all.at[d], ls.at[1]).start()

    @pl.when(s == 0)
    def _():
        start_own(act)

    @pl.when(s == 1)
    def _():
        start_own(cot)

    swaps = [remote(w.at[1], other.at[i], ss.at[13 + i], rs.at[13 + i], (d, 1 - s)) for i, w in enumerate((w_gate, w_in))]
    for copy in swaps:
        copy.start()

    def weight_sends():
        out = []
        for i, chip in enumerate((dg, xn, yn)):
            col = pl.ds(pl.multiple_of(chip * cols, LANES), cols)
            out.append(remote(w_gate.at[0, :, col], gate_in.at[d], ss.at[7 + i], rs.at[7 + i], (chip, s)))
            out.append(remote(w_in.at[0, :, col], in_in.at[d], ss.at[10 + i], rs.at[10 + i], (chip, s)))
        return out

    @pl.when(s == 0)
    def _():
        for copy in weight_sends():
            copy.start()

    owns = own_sends(act)
    fwd_y = remote(inp_all.at[xn, pl.ds(0, half)], inp_all.at[xn, pl.ds(0, half)], ss.at[2], rs.at[2], (yn, s))
    fwd_x = remote(inp_all.at[yn, pl.ds(half, half)], inp_all.at[yn, pl.ds(half, half)], ss.at[3], rs.at[3], (xn, s))
    owns[0].wait_recv()
    fwd_y.start()
    owns[1].wait_recv()
    fwd_x.start()
    for copy in owns:
        copy.wait_send()
    for copy in [fwd_y, fwd_x] + len_sends + swaps:
        copy.wait()
    own_lens.wait()
    pltpu.make_async_copy(act, inp_all.at[d], ls.at[1]).wait()

    @pl.when(s == 0)
    def _():
        for copy in weight_sends():
            copy.wait()


def share_rows(buf, d, s, xn, yn, ss, rs, half):
    lo, hi = pl.ds(0, half), pl.ds(half, half)

    def own(part, i):
        return [remote(buf.at[d, part], buf.at[d, part], ss.at[2 * i + n], rs.at[2 * i + n], (chip, s)) for n, chip in enumerate((xn, yn))]

    own_lo, own_hi = own(lo, 0), own(hi, 1)
    fwd_y = remote(buf.at[xn, lo], buf.at[xn, lo], ss.at[4], rs.at[4], (yn, s))
    fwd_x = remote(buf.at[yn, hi], buf.at[yn, hi], ss.at[5], rs.at[5], (xn, s))
    return own_lo, own_hi, fwd_y, fwd_x


def finish_share(share):
    own_lo, own_hi, fwd_y, fwd_x = share
    own_lo[0].wait_recv()
    fwd_y.start()
    own_hi[1].wait_recv()
    fwd_x.start()
    own_hi[0].wait_recv()
    own_lo[1].wait_recv()
    fwd_y.wait_recv()
    fwd_x.wait_recv()
    for copy in own_lo + own_hi + [fwd_y, fwd_x]:
        copy.wait_send()


def forward_kernel(sel, w_gate, w_in, w_out, gate_in, in_in, other,
                   wc, a_s, b_s, u_s, ho_s, no_s, r_s,
                   wv, wov, hb, nb, ub, zp, acc, ab, rv, ra1, rb1, ra2, rb2,
                   wss, wrs, hss, hrs, ass, ars, zss, zrs, lw, lo, lab, lsv, lh):
    d, s, xn, yn, dg = place()
    T = sel.shape[0]
    half = T // 2
    cols = wc.shape[4]
    tiles = cols // LANES
    dm = 512
    lo_rows, hi_rows = pl.ds(0, half), pl.ds(half, half)
    meet()

    pltpu.make_async_copy(w_out.at[0], wov, lo.at[0]).start()

    def column(chip):
        return pl.ds(pl.multiple_of(chip * cols, LANES), cols)

    def weight_sends(layer, src, core):
        out = []
        for i, chip in enumerate((dg, xn, yn)):
            for m in range(2):
                out.append(remote(src[m].at[:, column(chip)], wc.at[layer, m, d], wss.at[layer, m, i], wrs.at[layer, m, i], (chip, core)))
        return out

    other_pair = (other.at[0], other.at[1])
    first_pair = (w_gate.at[0], w_in.at[0])

    @pl.when(s == 1)
    def _():
        for copy in weight_sends(1, other_pair, 0) + weight_sends(0, first_pair, 1):
            copy.start()

    def in_copies():
        return [pltpu.make_async_copy(sel.at[:, pl.ds(c * dm, dm)], hb.at[0, c], lh.at[c]) for c in range(4)]

    def hand_over():
        return [remote(hb.at[2, c], hb.at[0, c], hss.at[i], hrs.at[i], (d, 1 - s)) for i, c in enumerate((d, xn, yn, dg))]

    @pl.when(s == 0)
    def _():
        for copy in in_copies():
            copy.start()
        for copy in in_copies():
            copy.wait()

    @pl.when(s == 1)
    def _():
        for copy in hand_over():
            copy.wait_recv()

    def load_weights(j):
        def body(k, carry):
            col = pl.ds(pl.multiple_of(k * LANES, LANES), LANES)
            own = pl.ds(pl.multiple_of(d * cols + k * LANES, LANES), LANES)
            for m, w in enumerate((w_gate, w_in)):
                pltpu.make_async_copy(w.at[j, :, own], wv.at[m, pl.ds(pl.multiple_of(d * dm, dm), dm), col], lw.at[k]).start()
                for chip in (xn, yn, dg):
                    dst = wv.at[m, pl.ds(pl.multiple_of(chip * dm, dm), dm), col]
                    if j == 0:
                        @pl.when(s == 0)
                        def _():
                            pltpu.make_async_copy((gate_in, in_in)[m].at[chip, :, col], dst, lw.at[k]).start()

                        @pl.when(s == 1)
                        def _():
                            pltpu.make_async_copy(wc.at[0, m, chip, :, col], dst, lw.at[k]).start()
                    else:
                        pltpu.make_async_copy(wc.at[1, m, chip, :, col], dst, lw.at[k]).start()
            return carry
        lax.fori_loop(0, tiles, body, 0)

    def wait_columns(j):
        for i, chip in enumerate((dg, xn, yn)):
            for m in range(2):
                remote(wc.at[j, m, chip], wc.at[j, m, chip], wss.at[j, m, i], wrs.at[j, m, i], (chip, s)).wait_recv()

    for j in range(2):
        if j == 0:
            @pl.when(s == 1)
            def _():
                wait_columns(0)
        else:
            wait_columns(1)
        load_weights(j)

        step = 32

        def norm_body(i, carry):
            rows = pl.ds(pl.multiple_of(i * step, step), step)
            blocks = [hb[j, c, rows, :].astype(F32) for c in range(4)]
            total = sum(jnp.sum(b * b, axis=-1, keepdims=True) for b in blocks)
            inv = lax.rsqrt(total * (1.0 / (4 * dm)) + EPSILON)
            for c in range(4):
                nb[rows, c * dm:(c + 1) * dm] = (blocks[c] * inv).astype(BF16)
            rv[j, rows, :] = jnp.broadcast_to(inv, (step, LANES))
            return carry
        lax.fori_loop(0, T // step, norm_body, 0)
        saves = [
            pltpu.make_async_copy(hb.at[j, d], ho_s.at[j], lsv.at[0]),
            pltpu.make_async_copy(nb.at[:, pl.ds(pl.multiple_of(d * dm, dm), dm)], no_s.at[j], lsv.at[1]),
            pltpu.make_async_copy(rv.at[j], r_s.at[j], lsv.at[2]),
        ]
        for copy in saves:
            copy.start()

        def ab_copies(k, slot):
            return [pltpu.make_async_copy(ab.at[slot, 0], a_s.at[j, k], lab.at[slot, 0]),
                    pltpu.make_async_copy(ab.at[slot, 1], b_s.at[j, k], lab.at[slot, 1])]

        def ab_body(k, carry):
            col = pl.ds(pl.multiple_of(k * LANES, LANES), LANES)
            pltpu.make_async_copy(wv.at[:, :, col], wv.at[:, :, col], lw.at[k]).wait()
            acc[...] = jnp.dot(nb[...], jnp.concatenate([wv[0, :, col], wv[1, :, col]], axis=1), preferred_element_type=F32)
            slot = lax.rem(k, 2)

            @pl.when(k >= 2)
            def _():
                for copy in ab_copies(k, slot):
                    copy.wait()
            a, b = acc[:, :LANES], acc[:, LANES:]
            ab[slot, 0] = a
            ab[slot, 1] = b
            ub[:, col] = (a * jax.nn.sigmoid(a) * b).astype(BF16)
            for copy in ab_copies(k, slot):
                copy.start()
            return carry
        lax.fori_loop(0, tiles, ab_body, 0)
        for k in (tiles - 2, tiles - 1):
            for copy in ab_copies(k, k % 2):
                copy.wait()
        save_u = pltpu.make_async_copy(ub, u_s.at[j], lsv.at[3])
        save_u.start()

        def mix():
            pltpu.make_async_copy(w_out.at[j], wov, lo.at[0]).wait()

            def block(c):
                zp[c] = jnp.dot(ub[...], wov[:, pl.ds(pl.multiple_of(c * dm, dm), dm)], preferred_element_type=F32)

            def send(i, c, rows, dst, chip):
                return remote(zp.at[c, rows], dst, zss.at[i], zrs.at[i], (chip, s))
            first = [send(0, dg, lo_rows, ra1.at[0], xn), send(1, dg, hi_rows, rb1.at[0], yn)]
            second = [send(2, xn, lo_rows, ra1.at[1], xn), send(3, yn, hi_rows, rb1.at[1], yn)]
            third = [send(4, yn, lo_rows, ra2, yn), send(5, xn, hi_rows, rb2, xn)]
            block(dg)
            for copy in first:
                copy.start()
            block(xn)
            second[0].start()
            block(yn)
            second[1].start()
            block(d)
            first[0].wait_recv()
            zp[yn, :half, :] += ra1[0]
            third[0].start()
            first[1].wait_recv()
            zp[xn, half:, :] += rb1[0]
            third[1].start()
            share = share_rows(hb.at[j + 1], d, s, xn, yn, ass, ars, half)
            for n, (rows, one, two) in enumerate(((lo_rows, ra1, ra2), (hi_rows, rb1, rb2))):
                second[n].wait_recv()
                third[n].wait_recv()
                branch = (zp[d, rows, :] + one[1] + two[...]).astype(BF16).astype(F32)
                hb[j + 1, d, rows, :] = (hb[j, d, rows, :].astype(F32) + branch).astype(BF16)
                for copy in share[n]:
                    copy.start()
            finish_share(share)
            for copy in first + second + third:
                copy.wait_send()

        if j == 0:
            mix()

            @pl.when(s == 0)
            def _():
                pltpu.make_async_copy(w_out.at[1], wov, lo.at[0]).start()
        else:
            @pl.when(s == 0)
            def _():
                mix()
                hands = hand_over()
                for copy in hands:
                    copy.start()
                sends = weight_sends(1, other_pair, 1)
                for copy in sends:
                    copy.start()
                for copy in hands + sends:
                    copy.wait_send()
        for copy in saves:
            copy.wait()
        save_u.wait()

    @pl.when(s == 1)
    def _():
        for copy in weight_sends(1, other_pair, 0) + weight_sends(0, first_pair, 1):
            copy.wait_send()


def backward_kernel(sel, w_gate, w_in, w_out, a_s, b_s, ho_s, r_s,
                    da_o, db_o, e_o, e_bot,
                    wgv, wiv, wov, eb, daf, ab, dn, hov, rv, sq, sv,
                    dss, drs, fss, frs, ess, ers, hss, hrs, sss, srs, lw, lab, lout, lh, le):
    d, s, xn, yn, dg = place()
    T = sel.shape[0]
    half = T // 2
    cols = daf.shape[3]
    dm = 512
    wide = 2 * LANES
    n_full = cols // wide
    tail = cols - n_full * wide
    pad = sq.shape[0]
    lo_rows, hi_rows = pl.ds(0, half), pl.ds(half, half)
    meet()

    def weight_loads(j):
        return [pltpu.make_async_copy(w_out.at[j], wov, lw.at[0]), pltpu.make_async_copy(w_gate.at[j], wgv, lw.at[1]),
                pltpu.make_async_copy(w_in.at[j], wiv, lw.at[2])]
    for copy in weight_loads(1):
        copy.start()

    def in_copies():
        return [pltpu.make_async_copy(sel.at[:, pl.ds(c * dm, dm)], eb.at[2, c], lh.at[c]) for c in range(4)]

    def hand_over():
        return [remote(eb.at[0, c], eb.at[2, c], hss.at[i], hrs.at[i], (d, 1 - s)) for i, c in enumerate((d, xn, yn, dg))]

    @pl.when(s == 1)
    def _():
        for copy in in_copies():
            copy.start()
        for copy in in_copies():
            copy.wait()

    for j in (1, 0):
        small = [pltpu.make_async_copy(ho_s.at[j], hov, le.at[0]), pltpu.make_async_copy(r_s.at[j], rv, le.at[1])]
        for copy in small:
            copy.start()

        def ab_loads(c, slot, width):
            out = []
            for n in range(width // LANES):
                for m, src in enumerate((a_s, b_s)):
                    out.append(pltpu.make_async_copy(src.at[j, 2 * c + n], ab.at[slot, m, n], lab.at[slot, m, n]))
            return out
        for copy in ab_loads(0, 0, wide):
            copy.start()
        if j == 1:
            @pl.when(s == 0)
            def _():
                for copy in hand_over():
                    copy.wait_recv()
        e_saves = [pltpu.make_async_copy(eb.at[j + 1, c], e_o.at[j, :, pl.ds(c * dm, dm)], le.at[2 + c]) for c in range(4)]
        for copy in e_saves:
            copy.start()
        weight_loads(j)[0].wait()

        def own_sends(c, col):
            out = []
            for m in range(2):
                for n, chip in enumerate((xn, yn)):
                    out.append(remote(daf.at[m, d, :, col], daf.at[m, d, :, col], dss.at[m, n, c], drs.at[m, n, c], (chip, s)))
            return out

        def forwards(c, col):
            return [remote(daf.at[0, xn, :, col], daf.at[0, xn, :, col], fss.at[1, c], frs.at[1, c], (yn, s)),
                    remote(daf.at[1, yn, :, col], daf.at[1, yn, :, col], fss.at[0, c], frs.at[0, c], (xn, s))]

        def columns(c, width):
            return pl.ds(pl.multiple_of(c * wide, LANES), width)

        def du_tile(c, slot, width):
            col = columns(c, width)
            e_all = jnp.concatenate([eb[j + 1, n] for n in range(4)], axis=1)
            dn[:, :width] = nt_dot(e_all, wov[col, :])
            for copy in ab_loads(c, slot, width):
                copy.wait()
            for n in range(width // LANES):
                lane = pl.ds(pl.multiple_of(c * wide + n * LANES, LANES), LANES)
                a, b, du = ab[slot, 0, n], ab[slot, 1, n], dn[:, n * LANES:(n + 1) * LANES]
                sig = jax.nn.sigmoid(a)
                daf[0, d, :, lane] = (du * b * sig * (1.0 + a * (1.0 - sig))).astype(BF16)
                daf[1, d, :, lane] = (du * (a * sig)).astype(BF16)
            for copy in own_sends(c, col):
                copy.start()

        def du_body(c, carry):
            slot = lax.rem(c, 2)

            @pl.when(c < n_full - 1)
            def _():
                for copy in ab_loads(c + 1, 1 - slot, wide):
                    copy.start()

            @pl.when(c == n_full - 1)
            def _():
                for copy in ab_loads(n_full, n_full % 2, tail):
                    copy.start()
            du_tile(c, slot, wide)
            return carry
        lax.fori_loop(0, n_full, du_body, 0)
        du_tile(n_full, n_full % 2, tail)

        outs = (da_o, db_o)

        def save_tile(m, chip, col, c, width):
            dst = outs[m].at[j, :, pl.ds(pl.multiple_of(chip * cols + c * wide, LANES), width)]
            pltpu.make_async_copy(daf.at[m, chip, :, col], dst, lout).start()

        def part(m, chip, c, width):
            col = columns(c, width)
            w = (wgv, wiv)[m]
            return nt_dot(daf[m, chip, :, col], w[:, pl.ds(pl.multiple_of(chip * cols + c * wide, LANES), width)])

        weight_loads(j)[1].wait()
        weight_loads(j)[2].wait()
        for m in range(2):
            save_tile(m, d, pl.ds(0, cols), 0, cols)

        def own_part(c, width, first):
            val = part(0, d, c, width) + part(1, d, c, width)
            dn[...] = val if first else dn[...] + val
        own_part(0, wide, True)
        lax.fori_loop(1, n_full, lambda c, carry: (own_part(c, wide, False), carry)[1], 0)
        own_part(n_full, tail, False)

        def near(c, width):
            col = columns(c, width)
            fwd_y, fwd_x = forwards(c, col)

            def came(m, n, chip):
                remote(daf.at[m, chip, :, col], daf.at[m, chip, :, col], dss.at[m, n, c], drs.at[m, n, c], (chip, s)).wait_recv()
            came(0, 0, xn)
            fwd_y.start()
            came(1, 1, yn)
            fwd_x.start()
            came(1, 0, xn)
            came(0, 1, yn)
            for chip in (xn, yn):
                for m in range(2):
                    save_tile(m, chip, col, c, width)
            dn[...] += (part(0, xn, c, width) + part(1, xn, c, width)) + (part(0, yn, c, width) + part(1, yn, c, width))
        lax.fori_loop(0, n_full, lambda c, carry: (near(c, wide), carry)[1], 0)
        near(n_full, tail)

        def far(c, width):
            col = columns(c, width)
            remote(daf.at[0, dg, :, col], daf.at[0, dg, :, col], fss.at[1, c], frs.at[1, c], (yn, s)).wait_recv()
            remote(daf.at[1, dg, :, col], daf.at[1, dg, :, col], fss.at[0, c], frs.at[0, c], (xn, s)).wait_recv()
            for m in range(2):
                save_tile(m, dg, col, c, width)
            dn[...] += part(0, dg, c, width) + part(1, dg, c, width)
        lax.fori_loop(0, n_full, lambda c, carry: (far(c, wide), carry)[1], 0)
        far(n_full, tail)
        if j == 1:
            for copy in weight_loads(0):
                copy.start()

        for copy in small:
            copy.wait()
        prod = dn[...] * hov[...].astype(F32)
        sq[:T, :] = (prod[:, :LANES] + prod[:, LANES:2 * LANES]) + (prod[:, 2 * LANES:3 * LANES] + prod[:, 3 * LANES:])
        sv[0] = jnp.broadcast_to(jnp.sum(sq[...].T, axis=0, keepdims=True), (8, pad))
        sums = [remote(sv.at[0], sv.at[1 + i], sss.at[i], srs.at[i], (chip, s)) for i, chip in enumerate((xn, yn, dg))]
        for copy in sums:
            copy.start()
        pltpu.make_async_copy(daf, daf, lout).wait()

        def drain(c, width):
            col = columns(c, width)
            for copy in own_sends(c, col) + forwards(c, col):
                copy.wait_send()
        lax.fori_loop(0, n_full, lambda c, carry: (drain(c, wide), carry)[1], 0)
        drain(n_full, tail)
        for copy in sums:
            copy.wait()
        mean = ((sv[0, 0:1, :] + sv[1, 0:1, :]) + (sv[2, 0:1, :] + sv[3, 0:1, :])) * (1.0 / (4 * dm))
        sq[...] = jnp.broadcast_to(mean, (LANES, pad)).T
        share = share_rows(eb.at[j], d, s, xn, yn, ess, ers, half)
        for n, base in enumerate((0, half)):
            rows = pl.ds(base, half)
            inv, avg = rv[rows, :], sq[rows, :]
            for c in range(4):
                lane = slice(c * LANES, (c + 1) * LANES)
                resid = inv * dn[rows, lane] - hov[rows, lane].astype(F32) * (inv * inv * inv) * avg
                eb[j, d, rows, lane] = (eb[j + 1, d, rows, lane].astype(F32) + resid).astype(BF16)
            for copy in share[n]:
                copy.start()
        finish_share(share)
        for copy in e_saves:
            copy.wait()

    def last_copies():
        return [pltpu.make_async_copy(eb.at[0, c], e_bot.at[:, pl.ds(c * dm, dm)], lh.at[c]) for c in range(4)]

    def last_sends():
        return [remote(eb.at[0, c], e_bot.at[:, pl.ds(c * dm, dm)], hss.at[4 + c], hrs.at[4 + c], (d, 1 - s)) for c in range(4)]

    @pl.when(s == 1)
    def _():
        hands = hand_over()
        for copy in hands:
            copy.start()
        for copy in hands:
            copy.wait_send()
        for copy in last_sends():
            copy.wait_recv()

    @pl.when(s == 0)
    def _():
        for copy in last_sends() + last_copies():
            copy.start()
        for copy in last_sends():
            copy.wait_send()
        for copy in last_copies():
            copy.wait()


ANY = pl.BlockSpec(memory_space=pl.ANY)
DMA = pltpu.SemaphoreType.DMA


def comm_call(kernel, name, cid, outs, n_in, scratch):
    return pl.pallas_call(
        kernel, name=name, out_shape=[jax.ShapeDtypeStruct(*o) for o in outs], in_specs=[ANY] * n_in, out_specs=[ANY] * len(outs),
        scratch_shapes=scratch, compiler_params=pltpu.CompilerParams(collective_id=cid, has_side_effects=True, vmem_limit_bytes=VMEM_LIMIT))


def gather_call(act, cot, lens, w_gate, w_in):
    rows, dmod = act.shape
    _, dsh, dff = w_gate.shape
    cols = dff // 4
    outs = [((4, rows, dmod), BF16), ((4,) + lens.shape, jnp.int32), ((4, dsh, cols), BF16), ((4, dsh, cols), BF16), ((2, dsh, dff), BF16)]
    return comm_call(gather_kernel, 'gather', 0, outs, 5, [DMA((15,)), DMA((15,)), DMA((2,))])(act, cot, lens, w_gate, w_in)


def forward_call(cid, sel, w_gate, w_in, w_out, gate_in, in_in, other):
    T, dmod = sel.shape
    _, dsh, dff = w_gate.shape
    cols = dff // 4
    half = T // 2
    tiles = cols // LANES
    outs = [((2, 2, 4, dsh, cols), BF16), ((2, tiles, T, LANES), F32), ((2, tiles, T, LANES), F32), ((2, T, cols), BF16),
            ((2, T, dsh), BF16), ((2, T, dsh), BF16), ((2, T, LANES), F32)]
    V = pltpu.VMEM
    scratch = [V((2, dmod, cols), BF16), V((cols, dmod), BF16), V((3, 4, T, dsh), BF16), V((T, dmod), BF16), V((T, cols), BF16),
               V((4, T, dsh), F32), V((T, 2 * LANES), F32), V((2, 2, T, LANES), F32), V((2, T, LANES), F32),
               V((2, half, dsh), F32), V((2, half, dsh), F32), V((half, dsh), F32), V((half, dsh), F32),
               DMA((2, 2, 3)), DMA((2, 2, 3)), DMA((4,)), DMA((4,)), DMA((6,)), DMA((6,)), DMA((6,)), DMA((6,)),
               DMA((tiles,)), DMA((1,)), DMA((2, 2)), DMA((4,)), DMA((4,))]
    return comm_call(forward_kernel, f'forward_{T}', cid, outs, 7, scratch)(sel, w_gate, w_in, w_out, gate_in, in_in, other)


def backward_call(cid, sel, w_gate, w_in, w_out, a_s, b_s, ho_s, r_s):
    T, dmod = sel.shape
    _, dsh, dff = w_gate.shape
    cols = dff // 4
    tiles = cols // LANES
    chunks = (tiles + 1) // 2
    pad = -(-T // LANES) * LANES
    outs = [((2, T, dff), BF16), ((2, T, dff), BF16), ((2, T, dmod), BF16), ((T, dmod), BF16)]
    V = pltpu.VMEM
    scratch = [V((dsh, dff), BF16), V((dsh, dff), BF16), V((cols, dmod), BF16), V((3, 4, T, dsh), BF16), V((2, 4, T, cols), BF16),
               V((2, 2, 2, T, LANES), F32), V((T, dsh), F32), V((T, dsh), BF16), V((T, LANES), F32), V((pad, LANES), F32), V((4, 8, pad), F32),
               DMA((2, 2, chunks)), DMA((2, 2, chunks)), DMA((2, chunks)), DMA((2, chunks)), DMA((6,)), DMA((6,)), DMA((8,)), DMA((8,)),
               DMA((3,)), DMA((3,)), DMA((3,)), DMA((2, 2, 2)), DMA, DMA((4,)), DMA((6,))]
    return comm_call(backward_kernel, f'backward_{T}', cid, outs, 8, scratch)(sel, w_gate, w_in, w_out, a_s, b_s, ho_s, r_s)


def solution(mesh, buckets=(992,)):
    act_spec = P(None, 'data')
    weight_spec = P('stage', None, 'data', None)

    def local_step(act_in, cot_out, seq_lens, w_gate, w_in, w_out):
        n_micro, n_rows, seq_len, dmod = act_in.shape
        rows = n_micro * n_rows * seq_len
        w_gate, w_in, w_out = w_gate[0], w_in[0], w_out[0]
        lens = jnp.zeros((8, LANES), jnp.int32).at[0, :n_micro].set(seq_lens[:, 0])
        inp_all, lens_all, gate_in, in_in, other = gather_call(act_in.reshape(rows, dmod), cot_out.reshape(rows, dmod), lens, w_gate, w_in)
        lens_all = lens_all[:, 0, :n_micro].reshape(-1)
        starts = jnp.cumsum(lens_all) - lens_all
        pos = jnp.arange(seq_len, dtype=jnp.int32)
        slot = jnp.where(pos[None, :] < lens_all[:, None], starts[:, None] + pos[None, :], -1).reshape(-1)
        count = jnp.sum(lens_all)

        def branch(which, T):
            def run(_):
                pick = (jnp.arange(T, dtype=jnp.int32)[:, None] == slot[None, :]).astype(BF16)
                sel = jnp.dot(pick, inp_all.reshape(-1, dmod), preferred_element_type=F32).astype(BF16)
                wc, a_s, b_s, u_s, ho_s, no_s, r_s = forward_call(1 + 2 * which, sel, w_gate, w_in, w_out, gate_in, in_in, other)
                da, db, e_o, e_bot = backward_call(2 + 2 * which, sel, w_gate, w_in, w_out, a_s, b_s, ho_s, r_s)
                own = lax.dynamic_slice_in_dim(slot, lax.axis_index('data') * rows, rows)
                back = (own[:, None] == jnp.arange(T, dtype=jnp.int32)[None, :]).astype(BF16)
                act_grad = jnp.dot(back, e_bot, preferred_element_type=F32).astype(BF16)

                def outer(left, right):
                    return lax.dot_general(left, right, (((1,), (1,)), ((0,), (0,))), preferred_element_type=F32)
                return act_grad.reshape(act_in.shape), outer(no_s, da)[None], outer(no_s, db)[None], outer(u_s, e_o)[None]
            return run
        if len(buckets) == 1:
            return branch(0, buckets[0])(0)
        which = sum((count > b).astype(jnp.int32) for b in buckets[:-1])
        return lax.switch(which, [branch(i, b) for i, b in enumerate(buckets)], 0)

    return jax.shard_map(local_step, mesh=mesh, in_specs=(act_spec, act_spec, act_spec, weight_spec, weight_spec, weight_spec), out_specs=(act_spec, weight_spec, weight_spec, weight_spec), check_vma=False)
```

time: 5510 us -> 1080 us (0.20)
  waiting for transfers between devices: 3650 us -> 0 us
  matrix products: 1400 us -> 75.7 us
  Pallas kernels: 0 us -> 995 us
  other arithmetic: 220 us -> 0.24 us
  local copies, waits for them, and re-layouts: 113 us -> 3.14 us
  starting transfers between devices: 78.6 us -> 0 us
    reduce_scatter x3 -> x0, waiting for transfers between devices: 2150 us -> none  [the longest x1 759 us: local_step(): lax.psum_scatter(jnp.stack(in_acc), 'data', scatter_dimension=1, tiled=True)]
    dot_general x88 -> x5, matrix products: 1400 us -> 75.7 us  [the longest x3 63.3 us: outer(): lax.dot_general(left, right, (((1,), (1,)), ((0,), (0,))), preferred_elem...]
    all_gather x3 -> x0, waiting for transfers between devices: 1200 us -> none  [the longest x1 400 us: local_step(): gate_full = lax.all_gather(w_gate[0], 'data', axis=1, tiled=True)]
    pallas_call x0 -> x3, Pallas kernels: none -> 995 us  [the longest x1 548 us: backward_call(): comm_call(backward_kernel, f'backward_{T}', cid, outs, 8, scratch)]
    ppermute x10 -> x0, waiting for transfers between devices: 301 us -> none  [the longest x5 296 us: bwd_step(): lax.ppermute(d_out, 'stage', bwd_perm)]
    another operation x3 -> x2, other arithmetic: 182 us -> 0.16 us  [the longest x1 61.3 us: local_step(): jnp.stack(in_acc)]
    another operation x6 -> x1, local copies, waits for them, and re-layouts: 91.2 us -> 0.08 us
    ppermute x10 -> x0, starting transfers between devices: 78.3 us -> none  [the longest x5 71.9 us: fwd_step(): return (lax.ppermute(h_out, 'stage', fwd_perm), act_stash)]
  transfers between devices with their start and end apart: 17 -> 0, of which waited for: 16 -> 0; matrix products, arithmetic and copies ran while one was open for 3% -> 0% of each run, Pallas kernels for 0% -> 0%
where the time goes in v1:
time: 1080 us; the launch traced here: 1070 us
  Pallas kernels  995 us (92%)
  matrix products  75.7 us (7%)
    pallas_call x1, Pallas kernels, backward_call(): comm_call(backward_kernel, f'backward_{T}', cid, outs, 8, scratch)  548 us
    pallas_call x1, Pallas kernels, forward_call(): comm_call(forward_kernel, f'forward_{T}', cid, outs, 7, scratch)  345 us
    pallas_call x1, Pallas kernels, gather_call(): comm_call(gather_kernel, 'gather', 0, outs, 5, [DMA((15,)), DMA((15,)), D...  102 us
    dot_general x3, matrix products, outer(): lax.dot_general(left, right, (((1,), (1,)), ((0,), (0,))), preferred_elem...  63.3 us

profile of v1, /device:TPU:0, one launch (start us, length us, event | category | flops | bytes accessed | tf_op | source)
XLA Modules:
  0.0 1074.5 jit_solution(8166994503734087662)
XLA Ops:
  0.6 1.3 scatter.4.lens
  1.9 102.0 %gather.1 = (bf16[4,256,2048]{2,1,0:T(8,128)(2,1)}, s32[4,8,128]{2,1,0:T(8,128)}, bf16[4,512,1408]{2,1,0:T(8,128)(2,1)}, bf16[4,512,1408]{2,1,0:T(8,128)(2,1)}, bf16[2,512,5632]{2,1,0:T(8,128)(2,1)}) custom-call(bf16[256,2048]{1,0:T(8,128)(2,1)} %bitcast.33, bf16[256,2048]{1,0:T(8,128)(2,1)} %bitcast.34, s32[8,128]{1,0:T(8,128)} %scatter.4.lens, ...), custom_call_target="tpu_custom_call" | custom-call | tf_op jit(solution)/shard_map/gather/pallas_call | solution.py:564
  103.9 0.7 slice_reduce_fusion
  104.6 0.1 reshape.126
  104.8 0.1 reduce.4
  104.9 0.1 lt.27
  105.0 0.1 add_select_fusion
  105.0 0.1 select_n.16
  105.1 0.0 copy-start
  105.1 8.0 fusion.1.sel
  113.2 0.0 copy-done
  113.2 344.9 %forward_992.1 = (bf16[2,2,4,512,1408]{4,3,2,1,0:T(8,128)(2,1)}, f32[2,11,992,128]{3,2,1,0:T(8,128)}, f32[2,11,992,128]{3,2,1,0:T(8,128)}, bf16[2,992,1408]{2,1,...) custom-call(bf16[992,2048]{1,0:T(8,128)(2,1)} %fusion.1.sel, ...), custom_call_target="tpu_custom_call" | custom-call | tf_op jit(solution)/shard_map/forward_992/pallas_call | solution.py:581
  458.1 547.7 %backward_992.1 = (bf16[2,992,5632]{2,1,0:T(8,128)(2,1)}, bf16[2,992,5632]{2,1,0:T(8,128)(2,1)}, bf16[2,992,2048]{2,1,0:T(8,128)(2,1)}, bf16[992,2048]{1,0:T(8,128)(2,1)}) custom-call(bf16[992,2048]{1,0:T(8,128)(2,1)} %fusion.1.sel, bf16[2,512,5632]{2,1,0:T(8,128)(2,1)} %bitcast.27, bf16[2,512,5632]{2,1,0:T(8,128)(2,1)} %bitcast.30, ...), custom_call_target="tpu_custom_call" | custom-call | tf_op jit(solution)/shard_map/backward_992/pallas_call | solution.py:597
  1005.7 0.0 copy-start.1
  1005.7 0.9 dynamic_slice.3
  1006.7 4.4 convolution_convert_fusion
  1011.1 0.0 copy-done.1
  1011.1 21.0 %convolution_bitcast_fusion.1 = f32[1,2,512,5632]{3,2,1,0:T(8,128)} fusion(bf16[2,992,512]{2,1,0:T(8,128)(2,1)S(1)} %copy-done.1, bf16[2,992,5632]{2,1,0:T(8,128)(2,1)} %get-tuple-element.42), kind=kOutput, calls=%fused_computation.1 | convolution fusion | flops 11442061312 | bytes 47448064 | tf_op jit(solution)/shard_map/dot_general | solution.py:627
  1032.1 21.4 %convolution_bitcast_fusion = f32[1,2,512,5632]{3,2,1,0:T(8,128)} fusion(bf16[2,992,512]{2,1,0:T(8,128)(2,1)S(1)} %copy-done.1, bf16[2,992,5632]{2,1,0:T(8,128)(2,1)} %get-tuple-element.43), kind=kOutput, calls=%fused_computation | convolution fusion | flops 11442061312 | bytes 47448064 | tf_op jit(solution)/shard_map/dot_general | solution.py:627
  1053.5 20.8 %convolution_bitcast_fusion.2 = f32[1,2,1408,2048]{3,2,1,0:T(8,128)} fusion(bf16[2,992,1408]{2,1,0:T(8,128)(2,1)} %get-tuple-element.44, bf16[2,992,2048]{2,1,0:T(8,128)(2,1)} %get-tuple-element.45), kind=kOutput, calls=%fused_computation.2 | convolution fusion | flops 11442061312 | bytes 36782080 | tf_op jit(solution)/shard_map/dot_general | solution.py:627
  (2 shorter events, 0.0 us)
Async XLA Ops:
  105.1 8.0 copy-start
  1005.7 5.3 copy-start.1
